TPU v7x, 256 devices: a whole 4x4x8 slice. The times are simulated.
256 devices in a mesh: shard: 64 (over z, y, core), tp: 4 (over x).
Axes of the slice: x: 4, y: 4, z: 8, core: 2. Of those that a mesh axis runs over, the one named last changes fastest.
Arguments:
- weight_query: bfloat16 [12288, 12288], P('shard', 'tp'), may hold values from -0.15625 to 0.15625
- low_query: bfloat16 [12288, 64], P('shard'), may hold values from -0.0546875 to 0.0546875
- high_query: bfloat16 [64, 12288], P(None, 'tp'), may hold values from -0.75 to 0.75
- weight_key: bfloat16 [12288, 12288], P('shard', 'tp'), may hold values from -0.15625 to 0.15625
- low_key: bfloat16 [12288, 64], P('shard'), may hold values from -0.0546875 to 0.0546875
- high_key: bfloat16 [64, 12288], P(None, 'tp'), may hold values from -0.75 to 0.75
- weight_value: bfloat16 [12288, 12288], P('shard', 'tp'), may hold values from -0.15625 to 0.15625
- low_value: bfloat16 [12288, 64], P('shard'), may hold values from -0.0546875 to 0.0546875
- high_value: bfloat16 [64, 12288], P(None, 'tp'), may hold values from -0.75 to 0.75
- norm_train: float32 [12288], P(('shard', 'tp')), may hold values from 0.25 to 1.75
- norm_step: float32 [12288], P(('shard', 'tp')), may hold values from -0.3 to 0.3
Outputs:
- ready_query: bfloat16 [12288, 12288], P(None, ('tp', 'shard'))
- ready_key: bfloat16 [12288, 12288], P(None, ('tp', 'shard'))
- ready_value: bfloat16 [12288, 12288], P(None, ('tp', 'shard'))
- column_query: float32 [12288], P(('tp', 'shard'))
- column_key: float32 [12288], P(('tp', 'shard'))
- column_value: float32 [12288], P(('tp', 'shard'))
- serve_norm: bfloat16 [12288], replicated
All inputs are finite; a program needn't handle non-finite values. Where the computation divides by a largest or mean magnitude, that divisor is 1e-20 or more.
Results may differ from a plain program's by a relative error of at most 0.001.
Values may be sent and summed in bfloat16 or wider, within the bound.
A program may use at most 64 MiB of HBM per device.

v0:
```python
import jax
import jax.numpy as jnp
from jax import lax
from jax.sharding import Mesh
from jax.sharding import PartitionSpec as P

D_MODEL = 12288
SHARD = ("shard_0", "shard_1", "shard_2")
SHARD_TP = ("shard_0", "shard_1", "shard_2", "tp")
TP_SHARD = ("tp", "shard_0", "shard_1", "shard_2")


mix_rate = 0.5


def split_up(array, dim, count):
    lengths = array.shape
    pieces = array.reshape(*lengths[:dim], count, lengths[dim] // count, *lengths[dim + 1 :])
    return jnp.moveaxis(pieces, dim, 0)


def sent_and_summed(array, axis, dim):
    pieces = split_up(array, dim, lax.axis_size(axis))
    arrived = lax.all_to_all(pieces, axis, split_axis=0, concat_axis=0, tiled=True)
    return arrived.sum(axis=0)


def filled_up(lines, count):
    spare = -len(lines) % count
    return jnp.pad(lines, [(0, spare)] + [(0, 0)] * (lines.ndim - 1))


def sent_to_all(array, axis):
    count = lax.axis_size(axis)
    return lax.all_to_all(
        jnp.broadcast_to(array[None], (count, *array.shape)), axis, 0, 0, tiled=True
    )


def joined_along(pieces, dim):
    pieces = jnp.moveaxis(pieces, 0, dim)
    lengths = pieces.shape
    return pieces.reshape(*lengths[:dim], lengths[dim] * lengths[dim + 1], *lengths[dim + 2 :])


def gathered_copies(array, axis, dim):
    pieces = sent_to_all(array, axis)
    return joined_along(pieces, dim)


def sum_by_parts(array, axes):
    own = sent_and_summed(filled_up(array, lax.axis_size(axes)), axes, 0)
    whole = gathered_copies(own, axes, 0)
    return whole[: len(array)].reshape(array.shape)


def in_one(arrays, axis):
    ends = [0]
    for a in arrays:
        ends.append(ends[-1] + a.size)
    so_far = sum_by_parts(jnp.concatenate([a.ravel() for a in arrays]), axis)
    return tuple((so_far[b:e].reshape(a.shape) for a, b, e in zip(arrays, ends, ends[1:])))


def whole_of(array, axes, dim):
    far, near = axes
    pieces = sent_to_all(sent_to_all(array, far), near)
    return joined_along(pieces.swapaxes(0, 1).reshape(-1, *array.shape), dim)


def body(
    weight_query,
    low_query,
    high_query,
    weight_key,
    low_key,
    high_key,
    weight_value,
    low_value,
    high_value,
    norm_train,
    norm_step,
):
    latest_query = weight_query.astype(jnp.float32) + mix_rate * jnp.dot(
        low_query, high_query, preferred_element_type=jnp.float32
    )
    latest_key = weight_key.astype(jnp.float32) + mix_rate * jnp.dot(
        low_key, high_key, preferred_element_type=jnp.float32
    )
    latest_value = weight_value.astype(jnp.float32) + mix_rate * jnp.dot(
        low_value, high_value, preferred_element_type=jnp.float32
    )
    total_query, total_key, total_value = in_one(
        (
            jnp.sum(jnp.abs(latest_query), axis=0),
            jnp.sum(jnp.abs(latest_key), axis=0),
            jnp.sum(jnp.abs(latest_value), axis=0),
        ),
        SHARD,
    )
    column_query = total_query / D_MODEL
    column_key = total_key / D_MODEL
    column_value = total_value / D_MODEL
    narrow_query, narrow_key, narrow_value = (
        (latest_query / column_query).astype(jnp.bfloat16),
        (latest_key / column_key).astype(jnp.bfloat16),
        (latest_value / column_value).astype(jnp.bfloat16),
    )
    ready_query, ready_key, ready_value = (
        lax.all_to_all(narrow_query, SHARD, split_axis=1, concat_axis=0, tiled=True),
        lax.all_to_all(narrow_key, SHARD, split_axis=1, concat_axis=0, tiled=True),
        lax.all_to_all(narrow_value, SHARD, split_axis=1, concat_axis=0, tiled=True),
    )
    place = lax.axis_index(SHARD)
    column_query = lax.dynamic_slice_in_dim(
        column_query, place * ready_query.shape[1], ready_query.shape[1]
    )
    column_key = lax.dynamic_slice_in_dim(
        column_key, place * ready_key.shape[1], ready_key.shape[1]
    )
    column_value = lax.dynamic_slice_in_dim(
        column_value, place * ready_value.shape[1], ready_value.shape[1]
    )
    serve_norm = whole_of(
        (norm_train + norm_step).astype(jnp.bfloat16),
        (("shard_0", "shard_1"), ("shard_2", "tp")),
        0,
    )
    return (ready_query, ready_key, ready_value, column_query, column_key, column_value, serve_norm)


def solution(mesh):
    torus = Mesh(
        mesh.devices.reshape(8, 4, 2, mesh.shape["tp"]), ("shard_0", "shard_1", "shard_2", "tp")
    )
    in_specs = (
        P(SHARD, "tp"),
        P(SHARD, None),
        P(None, "tp"),
        P(SHARD, "tp"),
        P(SHARD, None),
        P(None, "tp"),
        P(SHARD, "tp"),
        P(SHARD, None),
        P(None, "tp"),
        P(SHARD_TP),
        P(SHARD_TP),
    )
    out_specs = (
        P(None, TP_SHARD),
        P(None, TP_SHARD),
        P(None, TP_SHARD),
        P(TP_SHARD),
        P(TP_SHARD),
        P(TP_SHARD),
        P(),
    )
    return jax.shard_map(body, mesh=torus, in_specs=in_specs, out_specs=out_specs, check_vma=False)
```

profile of v0, /device:TPU:1, one launch (start us, length us, event | category | flops | bytes accessed | tf_op | source)
XLA Modules:
  0.0 209.1 jit_solution(6802979944682418986)
XLA Ops:
  0.6 0.0 copy-start
  0.6 0.0 copy-start.10
  0.7 0.0 copy-start.5
  0.7 0.0 copy-start.3
  0.7 1.0 copy-done
  1.6 1.9 abs_reduce_fusion.2
  3.6 0.0 copy-done.10
  3.6 0.0 copy-done.5
  3.6 0.0 copy-done.3
  3.6 0.0 copy-start.4
  3.6 0.0 copy-start.6
  3.6 0.0 copy-start.11
  3.6 2.0 abs_reduce_fusion
  5.7 0.0 copy-done.4
  5.7 0.0 copy-done.6
  5.7 0.0 copy-done.11
  5.7 0.0 copy-start.13
  5.7 2.0 abs_reduce_fusion.1
  7.7 0.8 all_to_all.59
  8.5 13.1 %all-to-all-start = ((f32[64,1,144]{2,1,0:T(1,128)}), f32[64,1,144]{2,1,0:T(1,128)S(1)}, u32[]{:S(2)}, u32[]{:S(2)}) async-start(f32[64,1,144]{2,1,0:T(1,128)} %all_to_all.59), calls=%async_computation | async-start | bytes 131072 | tf_op jit(solution)/shard_map/all_to_all | solution.py:24
  21.7 0.0 copy-done.12
  21.7 0.0 copy-done.13
  21.7 10.1 %all-to-all-done = f32[64,1,144]{2,1,0:T(1,128)S(1)} async-done(((f32[64,1,144]{2,1,0:T(1,128)}), f32[64,1,144]{2,1,0:T(1,128)S(1)}, u32[]{:S(2)}, u32[]{:S(2)}) %all-to-all-start) | async-done | bytes 36896 | tf_op jit(solution)/shard_map/all_to_all | solution.py:24
  31.7 0.6 broadcast_in_dim.9
  32.4 3.8 %all-to-all-start.5 = ((bf16[32,1,48]{2,1,0:T(2,128)(2,1)}), bf16[32,1,48]{2,1,0:T(2,128)(2,1)S(1)}, u32[]{:S(2)}, u32[]{:S(2)}) async-start(bf16[32,1,48]{2,1,0:T(2,128)(2,1)} %broadcast_in_dim.9), calls=%async_computation.5 | async-start | bytes 32768 | tf_op jit(solution)/shard_map/all_to_all | solution.py:35
  36.2 0.1 reduce_sum.39
  36.3 8.5 %all-to-all-done.5 = bf16[32,1,48]{2,1,0:T(2,128)(2,1)S(1)} async-done(((bf16[32,1,48]{2,1,0:T(2,128)(2,1)}), bf16[32,1,48]{2,1,0:T(2,128)(2,1)S(1)}, u32[]{:S(2)}, u32[]{:S(2)}) %all-to-all-start.5) | async-done | bytes 3104 | tf_op jit(solution)/shard_map/all_to_all | solution.py:35
  44.8 0.7 broadcast_in_dim.8
  45.4 5.6 %all-to-all-start.1 = ((f32[64,1,144]{2,1,0:T(1,128)}), f32[64,1,144]{2,1,0:T(1,128)S(1)}, u32[]{:S(2)}, u32[]{:S(2)}) async-start(f32[64,1,144]{2,1,0:T(1,128)} %broadcast_in_dim.8), calls=%async_computation.1 | async-start | bytes 131072 | tf_op jit(solution)/shard_map/all_to_all | solution.py:35
  51.0 0.7 reshape.50
  51.8 9.3 %all-to-all-done.1 = f32[64,1,144]{2,1,0:T(1,128)S(1)} async-done(((f32[64,1,144]{2,1,0:T(1,128)}), f32[64,1,144]{2,1,0:T(1,128)S(1)}, u32[]{:S(2)}, u32[]{:S(2)}) %all-to-all-start.1) | async-done | bytes 36896 | tf_op jit(solution)/shard_map/all_to_all | solution.py:35
  61.1 4.7 %all-to-all-start.6 = ((bf16[8,2,768]{2,1,0:T(2,128)(2,1)}), bf16[8,2,768]{2,1,0:T(2,128)(2,1)S(1)}, u32[]{:S(2)}, u32[]{:S(2)}) async-start(bf16[8,2,768]{2,1,0:T(2,128)(2,1)} %reshape.50), calls=%async_computation.6 | async-start | bytes 49152 | tf_op jit(solution)/shard_map/all_to_all | solution.py:35
  65.8 0.2 reduce.1
  66.0 0.1 reshape.48
  66.1 0.0 copy-start.9
  66.1 0.0 copy-start.8
  66.1 1.2 divide_convert_fusion.2
  67.3 2.7 %copy.45 = bf16[192,3072]{0,1:T(8,128)(2,1)} copy(bf16[192,3072]{1,0:T(8,128)(2,1)} %divide_convert_fusion.2) | data formatting | bytes 2359296 | tf_op jit(solution)/shard_map/convert_element_type | solution.py:105
  70.0 0.0 copy-done.9
  70.0 0.7 all-to-all-done.6
  70.7 5.3 %all-to-all-start.2 = ((bf16[192,64,48]{0,2,1:T(8,128)(2,1)}), bf16[192,64,48]{0,2,1:T(8,128)(2,1)}, u32[]{:S(2)}, u32[]{:S(2)}) async-start(bf16[192,64,48]{0,2,1:T(8,128)(2,1)} %bitcast.25), calls=%async_computation.2 | async-start | bytes 3145728 | tf_op jit(solution)/shard_map/all_to_all | solution.py:110
  76.0 0.0 copy-done.8
  76.0 0.0 copy-done.1
  76.0 3.5 %divide_convert_fusion = (bf16[192,3072]{1,0:T(8,128)(2,1)}, bf16[192,3072]{1,0:T(8,128)(2,1)}) fusion(f32[192,3072]{1,0:T(8,128)S(1)} %copy-done.1, f32[3072]{0:T(1024)S(1)} %get-tuple-element.7, f32[192,3072]{1,0:T(8,128)} %get-tuple-element.13, f32[3072]{0:T(1024)S(1)} %get-tuple-element.8), kind=kLoop, calls=%fused_computation.6 | loop fusion | flops 2359296 | bytes 7102464 | tf_op jit(solution)/shard_map/convert_element_type | solution.py:107
  79.6 2.6 %copy.47 = bf16[192,3072]{0,1:T(8,128)(2,1)} copy(bf16[192,3072]{1,0:T(8,128)(2,1)} %get-tuple-element.17) | data formatting | bytes 2359296 | tf_op jit(solution)/shard_map/convert_element_type | solution.py:106
  82.2 32.9 %all-to-all-done.2 = bf16[192,64,48]{0,2,1:T(8,128)(2,1)} async-done(((bf16[192,64,48]{0,2,1:T(8,128)(2,1)}), bf16[192,64,48]{0,2,1:T(8,128)(2,1)}, u32[]{:S(2)}, u32[]{:S(2)}) %all-to-all-start.2) | async-done | bytes 1179680 | tf_op jit(solution)/shard_map/all_to_all | solution.py:110
  115.1 6.4 %all-to-all-start.3 = ((bf16[192,64,48]{0,2,1:T(8,128)(2,1)}), bf16[192,64,48]{0,2,1:T(8,128)(2,1)S(1)}, u32[]{:S(2)}, u32[]{:S(2)}) async-start(bf16[192,64,48]{0,2,1:T(8,128)(2,1)} %bitcast.2), calls=%async_computation.3 | async-start | bytes 3145728 | tf_op jit(solution)/shard_map/all_to_all | solution.py:111
  121.5 0.0 copy-done.2
  121.5 1.6 copy.49
  123.1 37.5 %all-to-all-done.3 = bf16[192,64,48]{0,2,1:T(8,128)(2,1)S(1)} async-done(((bf16[192,64,48]{0,2,1:T(8,128)(2,1)}), bf16[192,64,48]{0,2,1:T(8,128)(2,1)S(1)}, u32[]{:S(2)}, u32[]{:S(2)}) %all-to-all-start.3) | async-done | bytes 1179680 | tf_op jit(solution)/shard_map/all_to_all | solution.py:111
  160.5 6.4 %all-to-all-start.4 = ((bf16[192,64,48]{0,2,1:T(8,128)(2,1)}), bf16[192,64,48]{0,2,1:T(8,128)(2,1)S(1)}, u32[]{:S(2)}, u32[]{:S(2)}) async-start(bf16[192,64,48]{0,2,1:T(8,128)(2,1)} %bitcast.24), calls=%async_computation.4 | async-start | bytes 3145728 | tf_op jit(solution)/shard_map/all_to_all | solution.py:112
  167.0 1.5 reshape.51
  168.4 1.5 copy.51
  169.9 1.6 reshape_reshape.3
  171.5 1.3 dynamic_slice.9
  172.8 1.3 dynamic_slice.10
  174.1 0.6 dynamic_slice.11
  174.7 3.1 %copy.46 = bf16[64,192,48]{1,0,2:T(8,128)(2,1)} copy(bf16[64,192,48]{1,2,0:T(8,128)(2,1)} %bitcast.1) | data formatting | bytes 2359296 | tf_op jit(solution)/shard_map/all_to_all | solution.py:110
  177.7 3.8 %all_to_all.65 = bf16[12288,48]{0,1:T(8,128)(2,1)} reshape(bf16[64,192,48]{1,0,2:T(8,128)(2,1)} %copy.46) | data formatting | bytes 2359296 | tf_op jit(solution)/shard_map/all_to_all | solution.py:110
  181.6 1.7 copy.48
  183.2 3.8 %all_to_all.69 = bf16[12288,48]{0,1:T(8,128)(2,1)} reshape(bf16[64,192,48]{1,0,2:T(8,128)(2,1)} %copy.48) | data formatting | bytes 2359296 | tf_op jit(solution)/shard_map/all_to_all | solution.py:111
  187.0 18.9 %all-to-all-done.4 = bf16[192,64,48]{0,2,1:T(8,128)(2,1)S(1)} async-done(((bf16[192,64,48]{0,2,1:T(8,128)(2,1)}), bf16[192,64,48]{0,2,1:T(8,128)(2,1)S(1)}, u32[]{:S(2)}, u32[]{:S(2)}) %all-to-all-start.4) | async-done | bytes 1179680 | tf_op jit(solution)/shard_map/all_to_all | solution.py:112
  206.0 0.5 copy.50
  206.5 2.5 %all_to_all.73 = bf16[12288,48]{0,1:T(8,128)(2,1)} reshape(bf16[64,192,48]{1,0,2:T(8,128)(2,1)S(1)} %copy.50) | data formatting | bytes 2359296 | tf_op jit(solution)/shard_map/all_to_all | solution.py:112
  (10 shorter events, 0.0 us)
Async XLA Ops:
  0.6 1.0 copy-start
  0.6 2.9 %copy-start.10 = (bf16[192,64]{0,1:T(8,128)(2,1)S(1)}, bf16[192,64]{0,1:T(8,128)(2,1)}, u32[]{:S(2)}) copy-start(bf16[192,64]{0,1:T(8,128)(2,1)} %param.18) | copy-start | bytes 73732
  0.7 2.9 %copy-start.5 = (bf16[64,3072]{1,0:T(8,128)(2,1)S(1)}, bf16[64,3072]{1,0:T(8,128)(2,1)}, u32[]{:S(2)}) copy-start(bf16[64,3072]{1,0:T(8,128)(2,1)} %param.19) | copy-start | bytes 1179652
  0.7 2.9 %copy-start.3 = (bf16[192,3072]{1,0:T(8,128)(2,1)S(1)}, bf16[192,3072]{1,0:T(8,128)(2,1)}, u32[]{:S(2)}) copy-start(bf16[192,3072]{1,0:T(8,128)(2,1)} %param.17) | copy-start | bytes 3538948
  3.6 2.1 copy-start.4
  3.6 2.1 copy-start.6
  3.6 2.1 copy-start.11
  5.7 16.0 %copy-start.12 = (f32[48]{0:T(128)S(1)}, f32[48]{0:T(128)}, u32[]{:S(2)}) copy-start(f32[48]{0:T(128)} %param.20) | copy-start | bytes 580
  5.7 16.0 %copy-start.13 = (f32[48]{0:T(128)S(1)}, f32[48]{0:T(128)}, u32[]{:S(2)}) copy-start(f32[48]{0:T(128)} %param.21) | copy-start | bytes 580
  8.5 23.2 %all-to-all-start = ((f32[64,1,144]{2,1,0:T(1,128)}), f32[64,1,144]{2,1,0:T(1,128)S(1)}, u32[]{:S(2)}, u32[]{:S(2)}) async-start(f32[64,1,144]{2,1,0:T(1,128)} %all_to_all.59), calls=%async_computation | async-start | bytes 131072 | tf_op jit(solution)/shard_map/all_to_all | solution.py:24
  32.4 12.4 %all-to-all-start.5 = ((bf16[32,1,48]{2,1,0:T(2,128)(2,1)}), bf16[32,1,48]{2,1,0:T(2,128)(2,1)S(1)}, u32[]{:S(2)}, u32[]{:S(2)}) async-start(bf16[32,1,48]{2,1,0:T(2,128)(2,1)} %broadcast_in_dim.9), calls=%async_computation.5 | async-start | bytes 32768 | tf_op jit(solution)/shard_map/all_to_all | solution.py:35
  45.4 15.7 %all-to-all-start.1 = ((f32[64,1,144]{2,1,0:T(1,128)}), f32[64,1,144]{2,1,0:T(1,128)S(1)}, u32[]{:S(2)}, u32[]{:S(2)}) async-start(f32[64,1,144]{2,1,0:T(1,128)} %broadcast_in_dim.8), calls=%async_computation.1 | async-start | bytes 131072 | tf_op jit(solution)/shard_map/all_to_all | solution.py:35
  61.1 9.6 %all-to-all-start.6 = ((bf16[8,2,768]{2,1,0:T(2,128)(2,1)}), bf16[8,2,768]{2,1,0:T(2,128)(2,1)S(1)}, u32[]{:S(2)}, u32[]{:S(2)}) async-start(bf16[8,2,768]{2,1,0:T(2,128)(2,1)} %reshape.50), calls=%async_computation.6 | async-start | bytes 49152 | tf_op jit(solution)/shard_map/all_to_all | solution.py:35
  66.1 3.9 %copy-start.9 = (f32[3072]{0:T(1024)}, f32[3072]{0:T(1024)S(1)}, u32[]{:S(2)}) copy-start(f32[3072]{0:T(1024)S(1)} %get-tuple-element.9) | copy-start | bytes 36868
  66.1 9.9 %copy-start.8 = (f32[3072]{0:T(1024)}, f32[3072]{0:T(1024)S(1)}, u32[]{:S(2)}) copy-start(f32[3072]{0:T(1024)S(1)} %get-tuple-element.8) | copy-start | bytes 36868
  67.3 8.7 %copy-start.1 = (f32[192,3072]{1,0:T(8,128)S(1)}, f32[192,3072]{1,0:T(8,128)}, u32[]{:S(2)}) copy-start(f32[192,3072]{1,0:T(8,128)} %get-tuple-element.11) | copy-start | bytes 7077892
  70.7 8.9 %copy-start.7 = (bf16[8,2,768]{2,1,0:T(2,128)(2,1)}, bf16[8,2,768]{2,1,0:T(2,128)(2,1)S(1)}, u32[]{:S(2)}) copy-start(bf16[8,2,768]{2,1,0:T(2,128)(2,1)S(1)} %all-to-all-done.6) | copy-start | bytes 73732
  70.7 44.4 %all-to-all-start.2 = ((bf16[192,64,48]{0,2,1:T(8,128)(2,1)}), bf16[192,64,48]{0,2,1:T(8,128)(2,1)}, u32[]{:S(2)}, u32[]{:S(2)}) async-start(bf16[192,64,48]{0,2,1:T(8,128)(2,1)} %bitcast.25), calls=%async_computation.2 | async-start | bytes 3145728 | tf_op jit(solution)/shard_map/all_to_all | solution.py:110
  79.6 41.9 %copy-start.2 = (bf16[192,3072]{1,0:T(8,128)(2,1)S(1)}, bf16[192,3072]{1,0:T(8,128)(2,1)}, u32[]{:S(2)}) copy-start(bf16[192,3072]{1,0:T(8,128)(2,1)} %get-tuple-element.16) | copy-start | bytes 3538948
  115.1 45.5 %all-to-all-start.3 = ((bf16[192,64,48]{0,2,1:T(8,128)(2,1)}), bf16[192,64,48]{0,2,1:T(8,128)(2,1)S(1)}, u32[]{:S(2)}, u32[]{:S(2)}) async-start(bf16[192,64,48]{0,2,1:T(8,128)(2,1)} %bitcast.2), calls=%async_computation.3 | async-start | bytes 3145728 | tf_op jit(solution)/shard_map/all_to_all | solution.py:111
  160.5 45.4 %all-to-all-start.4 = ((bf16[192,64,48]{0,2,1:T(8,128)(2,1)}), bf16[192,64,48]{0,2,1:T(8,128)(2,1)S(1)}, u32[]{:S(2)}, u32[]{:S(2)}) async-start(bf16[192,64,48]{0,2,1:T(8,128)(2,1)} %bitcast.24), calls=%async_computation.4 | async-start | bytes 3145728 | tf_op jit(solution)/shard_map/all_to_all | solution.py:112
where the time goes:
time: 210 us; the launch traced here: 209 us
  waiting for transfers between devices  118 us (56%)
  starting transfers between devices  45.3 us (22%)
  local copies, waits for them, and re-layouts  33.9 us (16%)
  matrix products  5.96 us (3%)
  other arithmetic  5.03 us (2%)
    all_to_all x1, waiting for transfers between devices, body(): lax.all_to_all(narrow_key, SHARD, split_axis=1, concat_axis=0, tiled=True)  37.5 us
    all_to_all x1, waiting for transfers between devices, body(): lax.all_to_all(narrow_query, SHARD, split_axis=1, concat_axis=0, tiled=True)  32.9 us
    all_to_all x1, waiting for transfers between devices, body(): lax.all_to_all(narrow_value, SHARD, split_axis=1, concat_axis=0, tiled=True)  18.9 us
    all_to_all x3, waiting for transfers between devices, sent_to_all(): lax.all_to_all(jnp.broadcast_to(array[None], (count, *array.shape)), axis...  18.6 us
    all_to_all x3, starting transfers between devices, sent_to_all(): lax.all_to_all(jnp.broadcast_to(array[None], (count, *array.shape)), axis...  14.1 us
    all_to_all x1, starting transfers between devices, sent_and_summed(): lax.all_to_all(pieces, axis, split_axis=0, concat_axis=0, tiled=True)  13.1 us
    all_to_all x1, waiting for transfers between devices, sent_and_summed(): lax.all_to_all(pieces, axis, split_axis=0, concat_axis=0, tiled=True)  10.1 us
    all_to_all x2, local copies, waits for them, and re-layouts, body(): lax.all_to_all(narrow_query, SHARD, split_axis=1, concat_axis=0, tiled=True)  6.9 us
  transfers between devices with their start and end apart: 7, of which 7 were waited for; matrix products, arithmetic and copies ran while one was open for 12% of the time, Pallas kernels for 0%

commit v1 on v0

v1 whole, which is shorter than its diff:
```python
import jax
import jax.numpy as jnp
from jax import lax
from jax.experimental import pallas as pl
from jax.experimental.pallas import tpu as pltpu
from jax.sharding import Mesh
from jax.sharding import PartitionSpec as P

D_MODEL = 12288
MIX_RATE = 0.5
MESH = pl.DeviceIdType.MESH
SIZES = {"z": 8, "y": 4, "c": 2, "x": 4}
ROWS = 192
TILE = 128
TILES = 9
UNITS = 36
Z_ORDER = (4, 3, 5, 2, 6, 1, 7)
PIECES = (
    ((0, 0, 0, 48), (1, 48, 0, 48), (2, 96, 0, 32)),
    ((2, 0, 32, 16), (3, 16, 0, 48), (4, 64, 0, 48), (5, 112, 0, 16)),
    ((5, 0, 16, 32), (6, 32, 0, 48), (7, 80, 0, 48)),
)
EARLY = 1


def shifted(**offsets):
    return {a: lax.rem(lax.axis_index(a) + o, SIZES[a]) for a, o in offsets.items()}


def all_peers():
    out = [{"z": dz, "c": dc} for dz in range(8) for dc in range(2) if dz or dc]
    out += [{"x": dx, "c": dc} for dx in range(1, 4) for dc in range(2)]
    out += [{"y": dy, "c": dc} for dy in range(1, 4) for dc in range(2)]
    return out


def remote(src, dst, send, recv, device):
    return pltpu.make_async_remote_copy(
        src_ref=src, dst_ref=dst, send_sem=send, recv_sem=recv, device_id=device, device_id_type=MESH
    )


def wait_bytes(ref, sem):
    pltpu.make_async_copy(ref, ref, sem).wait()


def product(low, high):
    return lax.dot_general(low, high, (((0,), (0,)), ((), ())), preferred_element_type=jnp.float32)


def kernel(
    wq, lq, hq, wk, lk, hk, wv, lv, hv, nt, ns,
    out, cols, norm,
    weights, highs, lows, units, ready, quarters, part, got1, got2, total, norms, gathered, mean, wide,
    w_sem, h_sem, l_sem, q_sem, own_sem,
    unit_sem, z_send, c_send,
    low_send, low_recv, low_send2, low_recv2,
    s1_send, s1_recv, s2_send, s2_recv, s3_send, s3_recv, n3_send, n3_recv, n4_send, n4_recv,
    y_send, y_recv,
):
    z, y, c, x = (lax.axis_index(a) for a in ("z", "y", "c", "x"))
    member = 2 * y + c
    w_in, l_in, h_in = (wq, wk, wv), (lq, lk, lv), (hq, hk, hv)

    barrier = pltpu.get_barrier_semaphore()
    peers = all_peers()
    for p in peers:
        pl.semaphore_signal(barrier, inc=1, device_id=shifted(**p), device_id_type=MESH)

    loads = []
    for t in range(3):
        loads.append(
            (
                pltpu.make_async_copy(w_in[t], weights.at[t], w_sem.at[t]),
                pltpu.make_async_copy(h_in[t], highs.at[t], h_sem.at[t]),
                pltpu.make_async_copy(l_in[t], lows.at[t], l_sem.at[t]),
            )
        )
        for copy in loads[t]:
            copy.start()
    quarter = quarters.at[4 * c + x, 0]
    quarter_loads = []
    for t in range(3):
        copy = pltpu.make_async_copy(
            l_in[t].at[pl.ds(pl.multiple_of(16 * x, 16), 16), :],
            quarter.at[pl.ds(16 * t, 16), :],
            q_sem.at[t],
        )
        copy.start()
        quarter_loads.append(copy)

    def slot_of(k, tile):
        return 4 * k + tile // 2 if tile < 8 else 32 + k // 2

    def half(slot, core):
        return units.at[pl.ds(pl.multiple_of(384 * slot + ROWS * core, 64), ROWS), :]

    def slab(k, tile):
        first = 384 * lax.rem(z + k, 8) + TILE * (tile % 3)
        return weights.at[tile // 3, :, pl.ds(pl.multiple_of(first, TILE), TILE)]

    def slab_in(tile):
        first = 384 * z + TILE * (tile % 3)
        return w_in[tile // 3].at[:, pl.ds(pl.multiple_of(first, TILE), TILE)]

    for tile in range(TILES):

        @pl.when(c == tile % 2)
        def _():
            slot = slot_of(0, tile)
            pltpu.make_async_copy(slab_in(tile), half(slot, c), unit_sem.at[slot]).start()

    for t in range(3):
        for copy in loads[t]:
            copy.wait()
        low = lows[t]

        def sums(s, _):
            for j in range(3):
                first = pl.ds(pl.multiple_of(384 * s + TILE * j, TILE), TILE)
                latest = weights[t, :, first].astype(jnp.float32) + MIX_RATE * product(low, highs[t, :, first])
                part[s, pl.ds(3 * t + j, 1), :] = jnp.sum(jnp.abs(latest), axis=0, keepdims=True)
            return 0

        lax.fori_loop(0, 8, sums, 0)
    own_norm = jnp.concatenate([nt[...] + ns[...], jnp.zeros((1, 80), jnp.float32)], axis=1)
    for s in range(8):
        part[s, pl.ds(9, 1), :] = own_norm
    for copy in quarter_loads:
        copy.wait()

    pl.semaphore_wait(barrier, len(peers))

    for k in Z_ORDER:
        remote(quarter, quarters.at[4 * c + x, k], low_send, low_recv, shifted(z=k)).start()
    for tile in range(TILES):

        @pl.when(c != tile % 2)
        def _():
            slot = slot_of(0, tile)
            remote(slab(0, tile), half(slot, c), c_send, unit_sem.at[slot], shifted(c=1)).start()

    def send_round(tile):
        for k in Z_ORDER:
            slot = slot_of(k, tile)
            device = {"z": lax.rem(z + k, 8), "c": (k + tile) % 2}
            remote(slab(k, tile), half(slot, c), z_send, unit_sem.at[slot], device).start()

    for tile in range(EARLY):
        send_round(tile)

    for dy in range(4):
        for dc in range(2):
            if dy or dc:
                to = shifted(y=dy, c=dc)
                remote(part.at[2 * to["y"] + to["c"]], got1.at[member], s1_send, s1_recv, to).start()
    got1[member] = part[member]
    wait_bytes(got1.at[pl.ds(0, 7)], s1_recv)
    mine = got1[0]
    for m in range(1, 8):
        mine = mine + got1[m]
    got2[0, pl.ds(0, 16), :] = mine
    for m in range(8):
        got2[0, pl.ds(16 + m, 1), :] = got1[m, pl.ds(9, 1), :]

    steps = lax.rem(member + 8 - z, 8)

    @pl.when(steps != 0)
    def _():
        remote(got2.at[0], got2.at[steps], s2_send, s2_recv, {"z": member}).start()

    for tile in range(EARLY, TILES):
        send_round(tile)

    wait_bytes(quarters.at[0, pl.ds(0, 7)], low_recv)
    for dx in range(4):
        for dc in range(2):
            if dx or dc:
                place = quarters.at[4 * c + x]
                remote(place, place, low_send2, low_recv2, shifted(x=dx, c=dc)).start()

    @pl.when(steps == 0)
    def _():
        wait_bytes(got2.at[pl.ds(0, 7)], s2_recv)
        whole = got2[0, pl.ds(0, 16), :]
        for k in range(1, 8):
            whole = whole + got2[k, pl.ds(0, 16), :]
        total[...] = whole
        for k in range(8):
            plane = lax.rem(z + 8 - k, 8)
            norms[x, pl.ds(pl.multiple_of(8 * plane, 8), 8), :] = got2[k, pl.ds(16, 8), :]
        for src, dst, send, recv in (
            (total, total, s3_send, s3_recv),
            (norms.at[x], norms.at[x], n3_send, n3_recv),
        ):
            n = 0
            for dy in range(4):
                for dc in range(2):
                    if dy or dc:
                        remote(src, dst, send.at[n], recv, shifted(y=dy, c=dc)).start()
                        n += 1

    @pl.when(steps != 0)
    def _():
        wait_bytes(total, s3_recv)
        wait_bytes(norms.at[x], n3_recv)

    for n, dx in enumerate((1, 2, 3)):
        remote(norms.at[x], norms.at[x], n4_send, n4_recv, shifted(x=dx)).start()
    mean[...] = total[...] / D_MODEL
    wait_bytes(quarters.at[pl.ds(0, 7)], low_recv2)

    def unit(n):
        i, j = n // 8, n % 8
        last = n >= 32
        k = jnp.where(last, 2 * (n - 32) + c, jnp.where(j < 4, 2 * j + c, 2 * (j - 4) + 1 - c))
        tile = jnp.where(last, 8, 2 * i + jnp.where(j < 4, 0, 1))
        slot = jnp.where(last, 32 + k // 2, 4 * k + i)
        return k, tile, slot

    def work(n):
        k, tile, slot = unit(n)
        tensor = tile // 3
        here = pl.ds(pl.multiple_of(384 * slot, 128), 384)
        wait_bytes(units.at[here, :], unit_sem.at[slot])
        first = 384 * z + TILE * (tile % 3)
        high = highs[tensor, :, pl.ds(pl.multiple_of(first, TILE), TILE)]
        rank = pl.ds(pl.multiple_of(16 * tensor, 16), 16)
        low = [
            jnp.concatenate([quarters[4 * core + q, k, rank, :] for q in range(4)], axis=0) for core in range(2)
        ]
        added = jnp.concatenate([product(a, high) for a in low], axis=0)
        latest = units[here, :].astype(jnp.float32) + MIX_RATE * added
        scaled = latest / mean[pl.ds(tile, 1), :]
        ready[pl.ds(pl.multiple_of(TILE * slot, TILE), TILE), :] = scaled.astype(jnp.bfloat16).T

    def hand_on(n):
        k, tile, slot = unit(n)
        tensor = tile // 3
        chip = 4 * lax.rem(z + 8 - k, 8) + y
        lanes = pl.ds(pl.multiple_of(384 * chip, 128), 384)
        for t in range(3):

            @pl.when(tile % 3 == t)
            def _():
                for owner, row, column, length in PIECES[t]:
                    src = ready.at[pl.ds(pl.multiple_of(TILE * slot + row, 16), length), :]
                    dst = out.at[tensor, pl.ds(column, length), lanes]

                    @pl.when(member == owner)
                    def _():
                        pltpu.make_async_copy(src, dst, y_recv.at[tensor]).start()

                    @pl.when(member != owner)
                    def _():
                        to = {"y": owner // 2, "c": owner % 2}
                        remote(src, dst, y_send, y_recv.at[tensor], to).start()

    def step(n, _):
        work(n)

        @pl.when(n > 0)
        def _():
            hand_on(n - 1)

        return 0

    lax.fori_loop(0, UNITS, step, 0)
    hand_on(UNITS - 1)

    for m in range(8):

        @pl.when(member == m)
        def _():
            for t in range(3):
                rows = [mean[pl.ds(3 * t + j, 1), :] for j in range(3)]
                line = jnp.concatenate(rows, axis=1)
                cols[pl.ds(t, 1), pl.ds(0, 48)] = line[:, 48 * m : 48 * m + 48]

    wait_bytes(norms.at[pl.ds(0, 3)], n4_recv)
    place = lax.broadcasted_iota(jnp.int32, (64, TILE), 1)
    n0, n1, n2, n3 = (norms[i] for i in range(4))
    r1, r2, r3 = pltpu.roll(n1, 48, 1), pltpu.roll(n2, 96, 1), pltpu.roll(n3, 16, 1)
    gathered[0] = jnp.where(place < 48, n0, jnp.where(place < 96, r1, r2))
    gathered[1] = jnp.where(place < 16, r2, r3)
    even, odd = pl.ds(0, 32, stride=2), pl.ds(1, 32, stride=2)
    a0, a1, b0, b1 = gathered[0, even, :], gathered[0, odd, :], gathered[1, even, :], gathered[1, odd, :]
    low_half = lax.broadcasted_iota(jnp.int32, (32, TILE), 1) < 64
    wide[pl.ds(0, 32, stride=3), :] = a0
    wide[pl.ds(1, 32, stride=3), :] = jnp.where(low_half, b0, pltpu.roll(a1, 64, 1))
    wide[pl.ds(2, 32, stride=3), :] = jnp.where(low_half, pltpu.roll(a1, 64, 1), pltpu.roll(b1, 64, 1))
    norm[...] = wide[...].astype(jnp.bfloat16)

    for t in range(3):
        wait_bytes(out.at[t], y_recv.at[t])
    wait_bytes(ready.at[pl.ds(0, 4032), :], y_send)
    wait_bytes(units.at[pl.ds(0, 63 * ROWS), :], z_send)

    @pl.when(c == 0)
    def _():
        wait_bytes(units.at[pl.ds(0, 4 * ROWS), :], c_send)

    @pl.when(c != 0)
    def _():
        wait_bytes(units.at[pl.ds(0, 5 * ROWS), :], c_send)

    wait_bytes(quarters.at[0, pl.ds(0, 7)], low_send)
    wait_bytes(quarters.at[pl.ds(0, 7)], low_send2)
    wait_bytes(got1.at[pl.ds(0, 7)], s1_send)
    wait_bytes(norms.at[pl.ds(0, 3)], n4_send)

    @pl.when(steps != 0)
    def _():
        wait_bytes(got2.at[0], s2_send)

    @pl.when(steps == 0)
    def _():
        for n in range(7):
            wait_bytes(total, s3_send.at[n])
            wait_bytes(norms.at[0], n3_send.at[n])


def body(wq, lq, hq, wk, lk, hk, wv, lv, hv, nt, ns):
    anywhere = pl.BlockSpec(memory_space=pl.ANY)
    local = pl.BlockSpec(memory_space=pltpu.VMEM)
    dma = pltpu.SemaphoreType.DMA
    bf16, f32 = jnp.bfloat16, jnp.float32
    out, cols, norm = pl.pallas_call(
        kernel,
        name="merge_and_place",
        out_shape=(
            jax.ShapeDtypeStruct((3, 48, D_MODEL), bf16),
            jax.ShapeDtypeStruct((8, TILE), f32),
            jax.ShapeDtypeStruct((96, TILE), bf16),
        ),
        in_specs=[anywhere] * 9 + [local] * 2,
        out_specs=(anywhere, local, local),
        scratch_shapes=[
            pltpu.VMEM((3, ROWS, 3072), bf16),
            pltpu.VMEM((3, 64, 3072), bf16),
            pltpu.VMEM((3, 64, ROWS), bf16),
            pltpu.VMEM((UNITS * 384, TILE), bf16),
            pltpu.VMEM((UNITS * TILE, 384), bf16),
            pltpu.VMEM((8, 8, 48, ROWS), bf16),
            pltpu.VMEM((8, 16, TILE), f32),
            pltpu.VMEM((8, 16, TILE), f32),
            pltpu.VMEM((8, 24, TILE), f32),
            pltpu.VMEM((16, TILE), f32),
            pltpu.VMEM((4, 64, TILE), f32),
            pltpu.VMEM((2, 64, TILE), f32),
            pltpu.VMEM((16, TILE), f32),
            pltpu.VMEM((96, TILE), f32),
            dma((3,)), dma((3,)), dma((3,)), dma((3,)), dma,
            dma((UNITS,)), dma, dma,
            dma, dma, dma, dma,
            dma, dma, dma, dma, dma((7,)), dma, dma((7,)), dma, dma, dma,
            dma, dma((3,)),
        ],
        compiler_params=pltpu.CompilerParams(collective_id=0, has_side_effects=True, vmem_limit_bytes=48 * 2**20),
    )(wq, lq.T, hq, wk, lk.T, hk, wv, lv.T, hv, nt.reshape(1, -1), ns.reshape(1, -1))
    return (
        out[0].T, out[1].T, out[2].T,
        cols[0, :48], cols[1, :48], cols[2, :48],
        norm.reshape(-1),
    )


def solution(mesh):
    torus = Mesh(mesh.devices.reshape(8, 4, 2, 4), ("z", "y", "c", "x"))
    shard = ("z", "y", "c")
    in_specs = (P(shard, "x"), P(shard, None), P(None, "x")) * 3 + (P((*shard, "x")),) * 2
    columns = ("x", *shard)
    out_specs = (P(None, columns),) * 3 + (P(columns),) * 3 + (P(),)
    return jax.shard_map(body, mesh=torus, in_specs=in_specs, out_specs=out_specs, check_vma=False)
```

time: 210 us -> 127 us (0.60)
  waiting for transfers between devices: 118 us -> 0 us
  Pallas kernels: 0 us -> 111 us
  starting transfers between devices: 45.3 us -> 0 us
  local copies, waits for them, and re-layouts: 33.9 us -> 15.3 us
  matrix products: 5.96 us -> 0 us
  other arithmetic: 5.03 us -> 0 us
    all_to_all x7 -> x0, waiting for transfers between devices: 118 us -> none  [the longest x1 37.5 us: body(): lax.all_to_all(narrow_key, SHARD, split_axis=1, concat_axis=0, tiled=True)]
    pallas_call x0 -> x1, Pallas kernels: none -> 111 us  [body(): pl.pallas_call(kernel, name='merge_and_place', out_shape=(jax.ShapeDtypeS...]
    all_to_all x7 -> x0, starting transfers between devices: 45.3 us -> none  [the longest x3 14.1 us: sent_to_all(): lax.all_to_all(jnp.broadcast_to(array[None], (count, *array.shape)), axis...]
    all_to_all x7 -> x0, local copies, waits for them, and re-layouts: 16.3 us -> none  [the longest x2 6.9 us: body(): lax.all_to_all(narrow_query, SHARD, split_axis=1, concat_axis=0, tiled=True)]
    unnamed x31 -> x23, local copies, waits for them, and re-layouts: 3.26 us -> 11 us
    convert_element_type x3 -> x0, local copies, waits for them, and re-layouts: 6.83 us -> none  [the longest x1 2.66 us: body(): (latest_query / column_query).astype(jnp.bfloat16)]
    dot_general x3 -> x0, matrix products: 5.96 us -> none  [the longest x1 2.04 us: body(): jnp.dot(low_value, high_value, preferred_element_type=jnp.float32)]
    convert_element_type x3 -> x0, other arithmetic: 4.76 us -> none  [the longest x1 3.55 us: body(): (latest_value / column_value).astype(jnp.bfloat16)]
  transfers between devices with their start and end apart: 7 -> 0, of which waited for: 7 -> 0; matrix products, arithmetic and copies ran while one was open for 12% -> 0% of each run, Pallas kernels for 0% -> 0%
where the time goes in v1:
time: 127 us
  Pallas kernels  111 us (87%)
  local copies, waits for them, and re-layouts  15.3 us (12%)
    pallas_call x1, Pallas kernels, body(): pl.pallas_call(kernel, name='merge_and_place', out_shape=(jax.ShapeDtypeS...  111 us
    unnamed x23, local copies, waits for them, and re-layouts  11 us
    transpose x1, local copies, waits for them, and re-layouts, body(): out[2]  3.85 us

profile of v1, /device:TPU:1, one launch (start us, length us, event | category | flops | bytes accessed | tf_op | source)
XLA Modules:
  0.0 126.6 jit_solution(17395000226166904861)
XLA Ops:
  0.6 0.0 copy-start
  0.6 1.3 copy-done
  1.9 0.0 copy-start.1
  1.9 1.3 %copy-done.1 = bf16[192,3072]{1,0:T(8,128)(2,1)S(1)} copy-done((bf16[192,3072]{1,0:T(8,128)(2,1)S(1)}, bf16[192,3072]{1,0:T(8,128)(2,1)}, u32[]{:S(2)}) %copy-start.1) | copy-done | bytes 1179672
  3.2 0.0 copy-start.2
  3.2 1.3 %copy-done.2 = bf16[192,3072]{1,0:T(8,128)(2,1)S(1)} copy-done((bf16[192,3072]{1,0:T(8,128)(2,1)S(1)}, bf16[192,3072]{1,0:T(8,128)(2,1)}, u32[]{:S(2)}) %copy-start.2) | copy-done | bytes 1179672
  4.5 0.0 copy-start.3
  4.5 1.0 copy-done.3
  5.4 0.0 copy-start.4
  5.4 1.0 copy-done.4
  6.4 0.0 copy-start.5
  6.4 1.0 copy-done.5
  7.4 0.0 copy-start.6
  7.4 0.8 copy-done.6
  8.2 0.0 copy-start.7
  8.2 0.8 copy-done.7
  9.0 0.0 copy-start.8
  9.0 0.8 copy-done.8
  9.7 0.0 copy-start.9
  9.7 0.7 copy-done.9
  10.4 0.0 copy-start.10
  10.4 0.7 copy-done.10
  11.0 110.6 %merge_and_place.1 = (bf16[3,48,12288]{2,1,0:T(8,128)(2,1)}, f32[8,128]{1,0:T(8,128)S(1)}, bf16[96,128]{1,0:T(8,128)(2,1)S(1)}) custom-call(bf16[192,3072]{1,0:T(8,128)(2,1)S(1)} %copy-done, bf16[64,192]{1,0:T(8,128)(2,1)S(1)} %bitcast.24, bf16[64,3072]{1,0:T(8,128)(2,1)S(1)} %copy-done.3, bf16[192,3072]{1,0:T(8,128)(2,1)S(1)} %copy-done.1, ...), custom_call_target="tpu_custom_call" | custom-call | tf_op jit(solution)/shard_map/merge_and_place/pallas_call | solution.py:328
  121.6 3.8 %slice_bitcast_fusion = (bf16[12288,48]{0,1:T(8,128)(2,1)}, bf16[12288,48]{0,1:T(8,128)(2,1)}, bf16[12288,48]{0,1:T(8,128)(2,1)}) fusion(bf16[3,48,12288]{2,1,0:T(8,128)(2,1)} %get-tuple-element.10), kind=kLoop, calls=%fused_computation | loop fusion | bytes 7077888 | tf_op jit(solution)/shard_map/transpose | solution.py:362
  125.4 0.5 slice_bitcast_fusion.3
  126.0 0.6 copy.19
Async XLA Ops:
  0.6 1.3 %copy-start = (bf16[192,3072]{1,0:T(8,128)(2,1)S(1)}, bf16[192,3072]{1,0:T(8,128)(2,1)}, u32[]{:S(2)}) copy-start(bf16[192,3072]{1,0:T(8,128)(2,1)} %wq.1) | copy-start | bytes 3538948
  1.9 1.3 %copy-start.1 = (bf16[192,3072]{1,0:T(8,128)(2,1)S(1)}, bf16[192,3072]{1,0:T(8,128)(2,1)}, u32[]{:S(2)}) copy-start(bf16[192,3072]{1,0:T(8,128)(2,1)} %wk.1) | copy-start | bytes 3538948
  3.2 1.3 %copy-start.2 = (bf16[192,3072]{1,0:T(8,128)(2,1)S(1)}, bf16[192,3072]{1,0:T(8,128)(2,1)}, u32[]{:S(2)}) copy-start(bf16[192,3072]{1,0:T(8,128)(2,1)} %wv.1) | copy-start | bytes 3538948
  4.5 1.0 copy-start.3
  5.4 1.0 copy-start.4
  6.4 1.0 copy-start.5
  7.4 0.8 copy-start.6
  8.2 0.8 copy-start.7
  9.0 0.8 copy-start.8
  9.7 0.7 copy-start.9
  10.4 0.7 copy-start.10

commit v2 on v1

--- a/solution.py
+++ b/solution.py
@@ -20,7 +20,7 @@
     ((2, 0, 32, 16), (3, 16, 0, 48), (4, 64, 0, 48), (5, 112, 0, 16)),
     ((5, 0, 16, 32), (6, 32, 0, 48), (7, 80, 0, 48)),
 )
-EARLY = 1
+EARLY = 2
 
 
 def shifted(**offsets):
@@ -51,8 +51,8 @@
 def kernel(
     wq, lq, hq, wk, lk, hk, wv, lv, hv, nt, ns,
     out, cols, norm,
-    weights, highs, lows, units, ready, quarters, part, got1, got2, total, norms, gathered, mean, wide,
-    w_sem, h_sem, l_sem, q_sem, own_sem,
+    weights, highs, lows, units, ready, quarters, part, got1, got2, total, norms, gathered, mean, wide, gain,
+    w_sem, h_sem, l_sem, q_sem, g_sem,
     unit_sem, z_send, c_send,
     low_send, low_recv, low_send2, low_recv2,
     s1_send, s1_recv, s2_send, s2_recv, s3_send, s3_recv, n3_send, n3_recv, n4_send, n4_recv,
@@ -78,6 +78,9 @@
         )
         for copy in loads[t]:
             copy.start()
+    gain_loads = [pltpu.make_async_copy(ref, gain.at[n], g_sem.at[n]) for n, ref in enumerate((nt, ns))]
+    for copy in gain_loads:
+        copy.start()
     quarter = quarters.at[4 * c + x, 0]
     quarter_loads = []
     for t in range(3):
@@ -89,29 +92,58 @@
         copy.start()
         quarter_loads.append(copy)
 
-    def slot_of(k, tile):
-        return 4 * k + tile // 2 if tile < 8 else 32 + k // 2
+    def tile_of(turn):
+        return lax.rem(turn + y, TILES)
+
+    def slot_of(k, turn):
+        return 4 * k + turn // 2 if turn < 8 else 32 + k // 2
 
     def half(slot, core):
         return units.at[pl.ds(pl.multiple_of(384 * slot + ROWS * core, 64), ROWS), :]
 
-    def slab(k, tile):
+    def slab(k, turn):
+        tile = tile_of(turn)
         first = 384 * lax.rem(z + k, 8) + TILE * (tile % 3)
         return weights.at[tile // 3, :, pl.ds(pl.multiple_of(first, TILE), TILE)]
 
-    def slab_in(tile):
+    for turn in range(TILES):
+        tile = tile_of(turn)
         first = 384 * z + TILE * (tile % 3)
-        return w_in[tile // 3].at[:, pl.ds(pl.multiple_of(first, TILE), TILE)]
-
-    for tile in range(TILES):
-
-        @pl.when(c == tile % 2)
+        for t in range(3):
+
+            @pl.when((c == turn % 2) & (tile // 3 == t))
+            def _():
+                slot = slot_of(0, turn)
+                src = w_in[t].at[:, pl.ds(pl.multiple_of(first, TILE), TILE)]
+                pltpu.make_async_copy(src, half(slot, c), unit_sem.at[slot]).start()
+
+    pl.semaphore_wait(barrier, len(peers))
+    for copy in quarter_loads:
+        copy.wait()
+    for t in range(3):
+        loads[t][0].wait()
+
+    for k in Z_ORDER:
+        remote(quarter, quarters.at[4 * c + x, k], low_send, low_recv, shifted(z=k)).start()
+    for turn in range(TILES):
+
+        @pl.when(c != turn % 2)
         def _():
-            slot = slot_of(0, tile)
-            pltpu.make_async_copy(slab_in(tile), half(slot, c), unit_sem.at[slot]).start()
-
-    for t in range(3):
-        for copy in loads[t]:
+            slot = slot_of(0, turn)
+            remote(slab(0, turn), half(slot, c), c_send, unit_sem.at[slot], shifted(c=1)).start()
+
+    def send_round(turn):
+        for k in Z_ORDER:
+            slot = slot_of(k, turn)
+            device = {"z": lax.rem(z + k, 8), "c": (k + turn) % 2}
+            remote(slab(k, turn), half(slot, c), z_send, unit_sem.at[slot], device).start()
+
+
+    for turn in range(EARLY):
+        send_round(turn)
+
+    for t in range(3):
+        for copy in loads[t][1:]:
             copy.wait()
         low = lows[t]
 
@@ -123,32 +155,11 @@
             return 0
 
         lax.fori_loop(0, 8, sums, 0)
-    own_norm = jnp.concatenate([nt[...] + ns[...], jnp.zeros((1, 80), jnp.float32)], axis=1)
+    for copy in gain_loads:
+        copy.wait()
+    own_norm = jnp.concatenate([gain[0] + gain[1], jnp.zeros((1, 80), jnp.float32)], axis=1)
     for s in range(8):
         part[s, pl.ds(9, 1), :] = own_norm
-    for copy in quarter_loads:
-        copy.wait()
-
-    pl.semaphore_wait(barrier, len(peers))
-
-    for k in Z_ORDER:
-        remote(quarter, quarters.at[4 * c + x, k], low_send, low_recv, shifted(z=k)).start()
-    for tile in range(TILES):
-
-        @pl.when(c != tile % 2)
-        def _():
-            slot = slot_of(0, tile)
-            remote(slab(0, tile), half(slot, c), c_send, unit_sem.at[slot], shifted(c=1)).start()
-
-    def send_round(tile):
-        for k in Z_ORDER:
-            slot = slot_of(k, tile)
-            device = {"z": lax.rem(z + k, 8), "c": (k + tile) % 2}
-            remote(slab(k, tile), half(slot, c), z_send, unit_sem.at[slot], device).start()
-
-    for tile in range(EARLY):
-        send_round(tile)
-
     for dy in range(4):
         for dc in range(2):
             if dy or dc:
@@ -169,8 +180,8 @@
     def _():
         remote(got2.at[0], got2.at[steps], s2_send, s2_recv, {"z": member}).start()
 
-    for tile in range(EARLY, TILES):
-        send_round(tile)
+    for turn in range(EARLY, TILES):
+        send_round(turn)
 
     wait_bytes(quarters.at[0, pl.ds(0, 7)], low_recv)
     for dx in range(4):
@@ -210,13 +221,20 @@
     mean[...] = total[...] / D_MODEL
     wait_bytes(quarters.at[pl.ds(0, 7)], low_recv2)
 
+    own = 5 - c
+
     def unit(n):
-        i, j = n // 8, n % 8
-        last = n >= 32
-        k = jnp.where(last, 2 * (n - 32) + c, jnp.where(j < 4, 2 * j + c, 2 * (j - 4) + 1 - c))
-        tile = jnp.where(last, 8, 2 * i + jnp.where(j < 4, 0, 1))
-        slot = jnp.where(last, 32 + k // 2, 4 * k + i)
-        return k, tile, slot
+        mine = n < own
+        m = jnp.where(mine, 0, n - own)
+        pair, place = m // 7, m % 7
+        first = place < 3 + c
+        index = jnp.where(first, place, place - 3 - c)
+        turn = jnp.where(mine, 2 * n + c, 2 * pair + jnp.where(first, 0, 1))
+        even = jnp.where(index == 0, 4, jnp.where(index == 1, 2, 6))
+        odd = jnp.where(index == 0, 3, jnp.where(index == 1, 5, jnp.where(index == 2, 1, 7)))
+        k = jnp.where(mine, 0, jnp.where((turn + c) % 2 == 0, even, odd))
+        slot = jnp.where(turn == 8, 32 + k // 2, 4 * k + turn // 2)
+        return k, tile_of(turn), slot
 
     def work(n):
         k, tile, slot = unit(n)
@@ -321,7 +339,7 @@
 
 
 def body(wq, lq, hq, wk, lk, hk, wv, lv, hv, nt, ns):
-    anywhere = pl.BlockSpec(memory_space=pl.ANY)
+    anywhere = pl.BlockSpec(memory_space=pltpu.HBM)
     local = pl.BlockSpec(memory_space=pltpu.VMEM)
     dma = pltpu.SemaphoreType.DMA
     bf16, f32 = jnp.bfloat16, jnp.float32
@@ -333,7 +351,7 @@
             jax.ShapeDtypeStruct((8, TILE), f32),
             jax.ShapeDtypeStruct((96, TILE), bf16),
         ),
-        in_specs=[anywhere] * 9 + [local] * 2,
+        in_specs=[anywhere] * 11,
         out_specs=(anywhere, local, local),
         scratch_shapes=[
             pltpu.VMEM((3, ROWS, 3072), bf16),
@@ -350,14 +368,15 @@
             pltpu.VMEM((2, 64, TILE), f32),
             pltpu.VMEM((16, TILE), f32),
             pltpu.VMEM((96, TILE), f32),
-            dma((3,)), dma((3,)), dma((3,)), dma((3,)), dma,
+            pltpu.VMEM((2, 1, 48), f32),
+            dma((3,)), dma((3,)), dma((3,)), dma((3,)), dma((2,)),
             dma((UNITS,)), dma, dma,
             dma, dma, dma, dma,
             dma, dma, dma, dma, dma((7,)), dma, dma((7,)), dma, dma, dma,
             dma, dma((3,)),
         ],
         compiler_params=pltpu.CompilerParams(collective_id=0, has_side_effects=True, vmem_limit_bytes=48 * 2**20),
-    )(wq, lq.T, hq, wk, lk.T, hk, wv, lv.T, hv, nt.reshape(1, -1), ns.reshape(1, -1))
+    )(*[pltpu.with_memory_space_constraint(a, pltpu.HBM) for a in (wq, lq.T, hq, wk, lk.T, hk, wv, lv.T, hv, nt.reshape(1, -1), ns.reshape(1, -1))])
     return (
         out[0].T, out[1].T, out[2].T,
         cols[0, :48], cols[1, :48], cols[2, :48],

time: 127 us -> 103 us (0.81)
  local copies, waits for them, and re-layouts: 15.3 us -> 3 us
  Pallas kernels: 111 us -> 99.4 us
    pallas_call x1, Pallas kernels: 111 us -> 99.4 us  [body(): pl.pallas_call(kernel, name='merge_and_place', out_shape=(jax.ShapeDtypeS...]
    unnamed x23 -> x1, local copies, waits for them, and re-layouts: 11 us -> 0.61 us
    transpose x1, local copies, waits for them, and re-layouts: 3.85 us -> 1.87 us  [body(): out[2]]
where the time goes in v2:
time: 103 us
  Pallas kernels  99.4 us (97%)
  local copies, waits for them, and re-layouts  3 us (3%)
    pallas_call x1, Pallas kernels, body(): pl.pallas_call(kernel, name='merge_and_place', out_shape=(jax.ShapeDtypeS...  99.4 us

profile of v2, /device:TPU:1, one launch (start us, length us, event | category | flops | bytes accessed | tf_op | source)
XLA Modules:
  0.0 103.0 jit_solution(3430900026428840373)
XLA Ops:
  0.6 99.4 %merge_and_place.1 = (bf16[3,48,12288]{2,1,0:T(8,128)(2,1)S(1)}, f32[8,128]{1,0:T(8,128)S(1)}, bf16[96,128]{1,0:T(8,128)(2,1)S(1)}) custom-call(bf16[192,3072]{1,0:T(8,128)(2,1)} %wq.1, bf16[64,192]{1,0:T(8,128)(2,1)} %bitcast.25, bf16[64,3072]{1,0:T(8,128)(2,1)} %hq.1, bf16[192,3072]{1,0:T(8,128)(2,1)} %wk.1, bf16[64,192]{1,0:T(8,128)(2,1)} %bitcast.26, ...), custom_call_target="tpu_custom_call" | custom-call | tf_op jit(solution)/shard_map/merge_and_place/pallas_call | solution.py:346
  100.0 1.9 %slice_bitcast_fusion = (bf16[12288,48]{0,1:T(8,128)(2,1)}, bf16[12288,48]{0,1:T(8,128)(2,1)}, bf16[12288,48]{0,1:T(8,128)(2,1)}) fusion(bf16[3,48,12288]{2,1,0:T(8,128)(2,1)S(1)} %get-tuple-element.10), kind=kLoop, calls=%fused_computation | loop fusion | bytes 7077888 | tf_op jit(solution)/shard_map/transpose | solution.py:381
  101.9 0.5 slice_bitcast_fusion.3
  102.4 0.6 copy.19

commit v3 on v2

--- a/solution.py
+++ b/solution.py
@@ -20,7 +20,6 @@
     ((2, 0, 32, 16), (3, 16, 0, 48), (4, 64, 0, 48), (5, 112, 0, 16)),
     ((5, 0, 16, 32), (6, 32, 0, 48), (7, 80, 0, 48)),
 )
-EARLY = 2
 
 
 def shifted(**offsets):
@@ -50,11 +49,11 @@
 
 def kernel(
     wq, lq, hq, wk, lk, hk, wv, lv, hv, nt, ns,
-    out, cols, norm,
+    out, col_q, col_k, col_v, norm,
     weights, highs, lows, units, ready, quarters, part, got1, got2, total, norms, gathered, mean, wide, gain,
     w_sem, h_sem, l_sem, q_sem, g_sem,
     unit_sem, z_send, c_send,
-    low_send, low_recv, low_send2, low_recv2,
+    low_send, low_recv, low_send2, low_recv2, low_send3, low_recv3,
     s1_send, s1_recv, s2_send, s2_recv, s3_send, s3_recv, n3_send, n3_recv, n4_send, n4_recv,
     y_send, y_recv,
 ):
@@ -93,7 +92,7 @@
         quarter_loads.append(copy)
 
     def tile_of(turn):
-        return lax.rem(turn + y, TILES)
+        return 3 * (turn // 3) + ((y + 1) // 2 + 8 - turn) % 3
 
     def slot_of(k, turn):
         return 4 * k + turn // 2 if turn < 8 else 32 + k // 2
@@ -102,20 +101,17 @@
         return units.at[pl.ds(pl.multiple_of(384 * slot + ROWS * core, 64), ROWS), :]
 
     def slab(k, turn):
-        tile = tile_of(turn)
-        first = 384 * lax.rem(z + k, 8) + TILE * (tile % 3)
-        return weights.at[tile // 3, :, pl.ds(pl.multiple_of(first, TILE), TILE)]
+        first = 384 * lax.rem(z + k, 8) + TILE * (tile_of(turn) % 3)
+        return weights.at[turn // 3, :, pl.ds(pl.multiple_of(first, TILE), TILE)]
 
     for turn in range(TILES):
-        tile = tile_of(turn)
-        first = 384 * z + TILE * (tile % 3)
-        for t in range(3):
-
-            @pl.when((c == turn % 2) & (tile // 3 == t))
-            def _():
-                slot = slot_of(0, turn)
-                src = w_in[t].at[:, pl.ds(pl.multiple_of(first, TILE), TILE)]
-                pltpu.make_async_copy(src, half(slot, c), unit_sem.at[slot]).start()
+        first = 384 * z + TILE * (tile_of(turn) % 3)
+
+        @pl.when(c == turn % 2)
+        def _():
+            slot = slot_of(0, turn)
+            src = w_in[turn // 3].at[:, pl.ds(pl.multiple_of(first, TILE), TILE)]
+            pltpu.make_async_copy(src, half(slot, c), unit_sem.at[slot]).start()
 
     pl.semaphore_wait(barrier, len(peers))
     for copy in quarter_loads:
@@ -123,8 +119,23 @@
     for t in range(3):
         loads[t][0].wait()
 
-    for k in Z_ORDER:
-        remote(quarter, quarters.at[4 * c + x, k], low_send, low_recv, shifted(z=k)).start()
+    def pass_low(k, step):
+        place = (k + step) % 8
+        lane = 4 * c + x
+        device = shifted(z=step % 8)
+        remote(quarters.at[lane, k], quarters.at[lane, place], low_send, low_recv.at[place], device).start()
+
+    def wait_low(k):
+        wait_bytes(quarters.at[0, k], low_recv.at[k])
+
+    def spread_low(*planes):
+        for k in planes:
+            place = quarters.at[4 * c + x, k]
+            for dx in (1, 2, 3):
+                remote(place, place, low_send2, low_recv2, shifted(x=dx)).start()
+
+    pass_low(0, 1)
+    pass_low(0, -1)
     for turn in range(TILES):
 
         @pl.when(c != turn % 2)
@@ -132,40 +143,76 @@
             slot = slot_of(0, turn)
             remote(slab(0, turn), half(slot, c), c_send, unit_sem.at[slot], shifted(c=1)).start()
 
-    def send_round(turn):
-        for k in Z_ORDER:
+    def send_round(turn, order=Z_ORDER):
+        for k in order:
             slot = slot_of(k, turn)
             device = {"z": lax.rem(z + k, 8), "c": (k + turn) % 2}
             remote(slab(k, turn), half(slot, c), z_send, unit_sem.at[slot], device).start()
 
 
-    for turn in range(EARLY):
-        send_round(turn)
+    send_round(0, Z_ORDER[:3])
+    wait_low(1)
+    wait_low(7)
+    pass_low(1, 1)
+    pass_low(7, -1)
+    send_round(0, Z_ORDER[3:])
+    spread_low(0, 1, 7)
+
+    def sum_up(t):
+        low = lows[t]
+
+        def sums(s, _):
+            first = pl.ds(pl.multiple_of(384 * s, TILE), 384)
+            latest = weights[t, :, first].astype(jnp.float32) + MIX_RATE * product(low[...], highs[t, :, first])
+            line = jnp.sum(jnp.abs(latest), axis=0, keepdims=True)
+            for j in range(3):
+                part[s, pl.ds(3 * t + j, 1), :] = line[:, TILE * j : TILE * (j + 1)]
+            return 0
+
+        lax.fori_loop(0, 8, sums, 0)
 
     for t in range(3):
         for copy in loads[t][1:]:
             copy.wait()
-        low = lows[t]
-
-        def sums(s, _):
-            for j in range(3):
-                first = pl.ds(pl.multiple_of(384 * s + TILE * j, TILE), TILE)
-                latest = weights[t, :, first].astype(jnp.float32) + MIX_RATE * product(low, highs[t, :, first])
-                part[s, pl.ds(3 * t + j, 1), :] = jnp.sum(jnp.abs(latest), axis=0, keepdims=True)
-            return 0
-
-        lax.fori_loop(0, 8, sums, 0)
     for copy in gain_loads:
         copy.wait()
     own_norm = jnp.concatenate([gain[0] + gain[1], jnp.zeros((1, 80), jnp.float32)], axis=1)
     for s in range(8):
         part[s, pl.ds(9, 1), :] = own_norm
+    sum_up(0)
+
+    wait_low(2)
+    wait_low(6)
+    pass_low(2, 1)
+    pass_low(6, -1)
+    send_round(1, Z_ORDER[:3])
+    spread_low(2, 6)
+
+    sum_up(1)
+
+    wait_low(3)
+    wait_low(5)
+
+    @pl.when(z % 2 == 1)
+    def _():
+        pass_low(3, 1)
+
+    @pl.when(z % 2 == 0)
+    def _():
+        pass_low(5, -1)
+
+    send_round(1, Z_ORDER[3:])
+    spread_low(3, 5)
+
+    sum_up(2)
+
     for dy in range(4):
         for dc in range(2):
             if dy or dc:
                 to = shifted(y=dy, c=dc)
                 remote(part.at[2 * to["y"] + to["c"]], got1.at[member], s1_send, s1_recv, to).start()
     got1[member] = part[member]
+    send_round(2, Z_ORDER[:2])
     wait_bytes(got1.at[pl.ds(0, 7)], s1_recv)
     mine = got1[0]
     for m in range(1, 8):
@@ -180,15 +227,15 @@
     def _():
         remote(got2.at[0], got2.at[steps], s2_send, s2_recv, {"z": member}).start()
 
-    for turn in range(EARLY, TILES):
+    wait_low(4)
+    spread_low(4)
+    send_round(2, Z_ORDER[2:])
+    for turn in range(3, TILES):
         send_round(turn)
 
-    wait_bytes(quarters.at[0, pl.ds(0, 7)], low_recv)
-    for dx in range(4):
-        for dc in range(2):
-            if dx or dc:
-                place = quarters.at[4 * c + x]
-                remote(place, place, low_send2, low_recv2, shifted(x=dx, c=dc)).start()
+    wait_bytes(quarters.at[pl.ds(0, 3)], low_recv2)
+    half_low = quarters.at[pl.ds(4 * c, 4)]
+    remote(half_low, half_low, low_send3, low_recv3, shifted(c=1)).start()
 
     @pl.when(steps == 0)
     def _():
@@ -219,7 +266,7 @@
     for n, dx in enumerate((1, 2, 3)):
         remote(norms.at[x], norms.at[x], n4_send, n4_recv, shifted(x=dx)).start()
     mean[...] = total[...] / D_MODEL
-    wait_bytes(quarters.at[pl.ds(0, 7)], low_recv2)
+    wait_bytes(quarters.at[pl.ds(0, 4)], low_recv3)
 
     own = 5 - c
 
@@ -293,7 +340,7 @@
             for t in range(3):
                 rows = [mean[pl.ds(3 * t + j, 1), :] for j in range(3)]
                 line = jnp.concatenate(rows, axis=1)
-                cols[pl.ds(t, 1), pl.ds(0, 48)] = line[:, 48 * m : 48 * m + 48]
+                (col_q, col_k, col_v)[t][...] = line[:, 48 * m : 48 * m + 48]
 
     wait_bytes(norms.at[pl.ds(0, 3)], n4_recv)
     place = lax.broadcasted_iota(jnp.int32, (64, TILE), 1)
@@ -323,7 +370,8 @@
         wait_bytes(units.at[pl.ds(0, 5 * ROWS), :], c_send)
 
     wait_bytes(quarters.at[0, pl.ds(0, 7)], low_send)
-    wait_bytes(quarters.at[pl.ds(0, 7)], low_send2)
+    wait_bytes(quarters.at[pl.ds(0, 3)], low_send2)
+    wait_bytes(quarters.at[pl.ds(0, 4)], low_send3)
     wait_bytes(got1.at[pl.ds(0, 7)], s1_send)
     wait_bytes(norms.at[pl.ds(0, 3)], n4_send)
 
@@ -336,6 +384,18 @@
         for n in range(7):
             wait_bytes(total, s3_send.at[n])
             wait_bytes(norms.at[0], n3_send.at[n])
+
+
+def settle(out, cq, ck, cv, norm, *results):
+    *to, sem = results
+    copies = [
+        pltpu.make_async_copy(src, dst, sem.at[n])
+        for n, (src, dst) in enumerate(zip((out.at[0], out.at[1], out.at[2], cq, ck, cv, norm), to))
+    ]
+    for copy in copies:
+        copy.start()
+    for copy in copies:
+        copy.wait()
 
 
 def body(wq, lq, hq, wk, lk, hk, wv, lv, hv, nt, ns):
@@ -343,16 +403,16 @@
     local = pl.BlockSpec(memory_space=pltpu.VMEM)
     dma = pltpu.SemaphoreType.DMA
     bf16, f32 = jnp.bfloat16, jnp.float32
-    out, cols, norm = pl.pallas_call(
+    out, *small = pl.pallas_call(
         kernel,
         name="merge_and_place",
         out_shape=(
             jax.ShapeDtypeStruct((3, 48, D_MODEL), bf16),
-            jax.ShapeDtypeStruct((8, TILE), f32),
+            *[jax.ShapeDtypeStruct((1, 48), f32)] * 3,
             jax.ShapeDtypeStruct((96, TILE), bf16),
         ),
         in_specs=[anywhere] * 11,
-        out_specs=(anywhere, local, local),
+        out_specs=(anywhere, local, local, local, local),
         scratch_shapes=[
             pltpu.VMEM((3, ROWS, 3072), bf16),
             pltpu.VMEM((3, 64, 3072), bf16),
@@ -371,17 +431,27 @@
             pltpu.VMEM((2, 1, 48), f32),
             dma((3,)), dma((3,)), dma((3,)), dma((3,)), dma((2,)),
             dma((UNITS,)), dma, dma,
-            dma, dma, dma, dma,
+            dma, dma((8,)), dma, dma, dma, dma,
             dma, dma, dma, dma, dma((7,)), dma, dma((7,)), dma, dma, dma,
             dma, dma((3,)),
         ],
         compiler_params=pltpu.CompilerParams(collective_id=0, has_side_effects=True, vmem_limit_bytes=48 * 2**20),
     )(*[pltpu.with_memory_space_constraint(a, pltpu.HBM) for a in (wq, lq.T, hq, wk, lk.T, hk, wv, lv.T, hv, nt.reshape(1, -1), ns.reshape(1, -1))])
-    return (
-        out[0].T, out[1].T, out[2].T,
-        cols[0, :48], cols[1, :48], cols[2, :48],
-        norm.reshape(-1),
-    )
+    either = pl.BlockSpec(memory_space=pl.ANY)
+    q, k, v, cq, ck, cv, norm = pl.pallas_call(
+        settle,
+        name="settle",
+        out_shape=(
+            *[jax.ShapeDtypeStruct((48, D_MODEL), bf16)] * 3,
+            *[jax.ShapeDtypeStruct((1, 48), f32)] * 3,
+            jax.ShapeDtypeStruct((96, TILE), bf16),
+        ),
+        in_specs=[either] * 5,
+        out_specs=[either] * 7,
+        scratch_shapes=[dma((7,))],
+        compiler_params=pltpu.CompilerParams(vmem_limit_bytes=2**20),
+    )(out, *small)
+    return q.T, k.T, v.T, cq.reshape(-1), ck.reshape(-1), cv.reshape(-1), norm.reshape(-1)
 
 
 def solution(mesh):

time: 103 us -> 97.7 us (0.949)
  local copies, waits for them, and re-layouts: 3 us -> 0 us
  Pallas kernels: 99.4 us -> 96.6 us
    pallas_call x1, Pallas kernels: 99.4 us -> 94.7 us  [body(): pl.pallas_call(kernel, name='merge_and_place', out_shape=(jax.ShapeDtypeS...]
    transpose x1 -> x0, local copies, waits for them, and re-layouts: 1.87 us -> none  [body(): out[2]]
    pallas_call x0 -> x1, Pallas kernels: none -> 1.86 us  [body(): pl.pallas_call(settle, name='settle', out_shape=(*[jax.ShapeDtypeStruct((...]
where the time goes in v3:
time: 97.7 us; the launch traced here: 97.2 us
  Pallas kernels  96.6 us (99%)
    pallas_call x1, Pallas kernels, body(): pl.pallas_call(kernel, name='merge_and_place', out_shape=(jax.ShapeDtypeS...  94.7 us

profile of v3, /device:TPU:1, one launch (start us, length us, event | category | flops | bytes accessed | tf_op | source)
XLA Modules:
  0.0 97.2 jit_solution(17667970196332519521)
XLA Ops:
  0.6 94.7 %merge_and_place.1 = (bf16[3,48,12288]{2,1,0:T(8,128)(2,1)S(1)}, f32[1,48]{1,0:T(1,128)S(1)}, f32[1,48]{1,0:T(1,128)S(1)}, f32[1,48]{1,0:T(1,128)S(1)}, bf16[96,128]{1,0:T(8,128)(2,1)S(1)}) custom-call(bf16[192,3072]{1,0:T(8,128)(2,1)} %wq.1, bf16[64,192]{1,0:T(8,128)(2,1)} %bitcast.12, bf16[64,3072]{1,0:T(8,128)(2,1)} %hq.1, bf16[192,3072]{1,0:T(8,128)(2,1)} %wk.1, ...), custom_call_target="tpu_custom_call" | custom-call | tf_op jit(solution)/shard_map/merge_and_place/pallas_call | solution.py:406
  95.4 1.9 %settle.1 = (bf16[48,12288]{1,0:T(8,128)(2,1)}, bf16[48,12288]{1,0:T(8,128)(2,1)}, bf16[48,12288]{1,0:T(8,128)(2,1)}, f32[1,48]{1,0:T(1,128)}, f32[1,48]{1,0:T(1...) custom-call(bf16[3,48,12288]{2,1,0:T(8,128)(2,1)S(1)} %get-tuple-element.19.out, f32[1,48]{1,0:T(1,128)S(1)} %get-tuple-element.20.cq, ...), custom_call_target="tpu_custom_call" | custom-call | tf_op jit(solution)/shard_map/settle/pallas_call | solution.py:441

commit v4 on v3

--- a/solution.py
+++ b/solution.py
@@ -14,7 +14,7 @@
 TILE = 128
 TILES = 9
 UNITS = 36
-Z_ORDER = (4, 3, 5, 2, 6, 1, 7)
+Z_ORDER = (1, 7, 3, 5, 2, 6, 4)
 PIECES = (
     ((0, 0, 0, 48), (1, 48, 0, 48), (2, 96, 0, 32)),
     ((2, 0, 32, 16), (3, 16, 0, 48), (4, 64, 0, 48), (5, 112, 0, 16)),
@@ -146,16 +146,16 @@
     def send_round(turn, order=Z_ORDER):
         for k in order:
             slot = slot_of(k, turn)
-            device = {"z": lax.rem(z + k, 8), "c": (k + turn) % 2}
+            device = {"z": lax.rem(z + k, 8), "c": (k + k // 4 + turn) % 2}
             remote(slab(k, turn), half(slot, c), z_send, unit_sem.at[slot], device).start()
 
 
-    send_round(0, Z_ORDER[:3])
+    send_round(0, Z_ORDER[:4])
     wait_low(1)
     wait_low(7)
     pass_low(1, 1)
     pass_low(7, -1)
-    send_round(0, Z_ORDER[3:])
+    send_round(0, Z_ORDER[4:])
     spread_low(0, 1, 7)
 
     def sum_up(t):
@@ -181,29 +181,7 @@
         part[s, pl.ds(9, 1), :] = own_norm
     sum_up(0)
 
-    wait_low(2)
-    wait_low(6)
-    pass_low(2, 1)
-    pass_low(6, -1)
-    send_round(1, Z_ORDER[:3])
-    spread_low(2, 6)
-
     sum_up(1)
-
-    wait_low(3)
-    wait_low(5)
-
-    @pl.when(z % 2 == 1)
-    def _():
-        pass_low(3, 1)
-
-    @pl.when(z % 2 == 0)
-    def _():
-        pass_low(5, -1)
-
-    send_round(1, Z_ORDER[3:])
-    spread_low(3, 5)
-
     sum_up(2)
 
     for dy in range(4):
@@ -211,8 +189,15 @@
             if dy or dc:
                 to = shifted(y=dy, c=dc)
                 remote(part.at[2 * to["y"] + to["c"]], got1.at[member], s1_send, s1_recv, to).start()
+
+    wait_low(2)
+    wait_low(6)
+    pass_low(2, 1)
+    pass_low(6, -1)
+    send_round(1, Z_ORDER[:4])
+    spread_low(2, 6)
+
     got1[member] = part[member]
-    send_round(2, Z_ORDER[:2])
     wait_bytes(got1.at[pl.ds(0, 7)], s1_recv)
     mine = got1[0]
     for m in range(1, 8):
@@ -227,11 +212,23 @@
     def _():
         remote(got2.at[0], got2.at[steps], s2_send, s2_recv, {"z": member}).start()
 
+    send_round(1, Z_ORDER[4:])
+    wait_low(3)
+    wait_low(5)
+
+    @pl.when(z % 2 == 1)
+    def _():
+        pass_low(3, 1)
+
+    @pl.when(z % 2 == 0)
+    def _():
+        pass_low(5, -1)
+
+    for turn in range(2, TILES):
+        send_round(turn)
+    spread_low(3, 5)
     wait_low(4)
     spread_low(4)
-    send_round(2, Z_ORDER[2:])
-    for turn in range(3, TILES):
-        send_round(turn)
 
     wait_bytes(quarters.at[pl.ds(0, 3)], low_recv2)
     half_low = quarters.at[pl.ds(4 * c, 4)]
@@ -277,9 +274,9 @@
         first = place < 3 + c
         index = jnp.where(first, place, place - 3 - c)
         turn = jnp.where(mine, 2 * n + c, 2 * pair + jnp.where(first, 0, 1))
-        even = jnp.where(index == 0, 4, jnp.where(index == 1, 2, 6))
-        odd = jnp.where(index == 0, 3, jnp.where(index == 1, 5, jnp.where(index == 2, 1, 7)))
-        k = jnp.where(mine, 0, jnp.where((turn + c) % 2 == 0, even, odd))
+        one = jnp.where(index == 0, 7, jnp.where(index == 1, 5, 2))
+        other = jnp.where(index == 0, 1, jnp.where(index == 1, 3, jnp.where(index == 2, 6, 4)))
+        k = jnp.where(mine, 0, jnp.where((turn + c) % 2 == 0, one, other))
         slot = jnp.where(turn == 8, 32 + k // 2, 4 * k + turn // 2)
         return k, tile_of(turn), slot
 

time: 97.7 us -> 96.2 us (0.985)
  Pallas kernels: 96.6 us -> 94.5 us
    pallas_call x1, Pallas kernels: 94.7 us -> 92.6 us  [body(): pl.pallas_call(kernel, name='merge_and_place', out_shape=(jax.ShapeDtypeS...]
where the time goes in v4:
time: 96.2 us; the launch traced here: 95.2 us
  Pallas kernels  94.5 us (98%)
    pallas_call x1, Pallas kernels, body(): pl.pallas_call(kernel, name='merge_and_place', out_shape=(jax.ShapeDtypeS...  92.6 us

profile of v4, /device:TPU:1, one launch (start us, length us, event | category | flops | bytes accessed | tf_op | source)
XLA Modules:
  0.0 95.2 jit_solution(9040169627873823248)
XLA Ops:
  0.6 92.6 %merge_and_place.1 = (bf16[3,48,12288]{2,1,0:T(8,128)(2,1)S(1)}, f32[1,48]{1,0:T(1,128)S(1)}, f32[1,48]{1,0:T(1,128)S(1)}, f32[1,48]{1,0:T(1,128)S(1)}, bf16[96,128]{1,0:T(8,128)(2,1)S(1)}) custom-call(bf16[192,3072]{1,0:T(8,128)(2,1)} %wq.1, bf16[64,192]{1,0:T(8,128)(2,1)} %bitcast.12, bf16[64,3072]{1,0:T(8,128)(2,1)} %hq.1, bf16[192,3072]{1,0:T(8,128)(2,1)} %wk.1, ...), custom_call_target="tpu_custom_call" | custom-call | tf_op jit(solution)/shard_map/merge_and_place/pallas_call | solution.py:403
  93.3 1.9 %settle.1 = (bf16[48,12288]{1,0:T(8,128)(2,1)}, bf16[48,12288]{1,0:T(8,128)(2,1)}, bf16[48,12288]{1,0:T(8,128)(2,1)}, f32[1,48]{1,0:T(1,128)}, f32[1,48]{1,0:T(1...) custom-call(bf16[3,48,12288]{2,1,0:T(8,128)(2,1)S(1)} %get-tuple-element.19.out, f32[1,48]{1,0:T(1,128)S(1)} %get-tuple-element.20.cq, ...), custom_call_target="tpu_custom_call" | custom-call | tf_op jit(solution)/shard_map/settle/pallas_call | solution.py:438

commit v5 on v4

--- a/solution.py
+++ b/solution.py
@@ -14,7 +14,7 @@
 TILE = 128
 TILES = 9
 UNITS = 36
-Z_ORDER = (1, 7, 3, 5, 2, 6, 4)
+Z_ORDER = (2, 6, 3, 5, 1, 7, 4)
 PIECES = (
     ((0, 0, 0, 48), (1, 48, 0, 48), (2, 96, 0, 32)),
     ((2, 0, 32, 16), (3, 16, 0, 48), (4, 64, 0, 48), (5, 112, 0, 16)),
@@ -274,8 +274,8 @@
         first = place < 3 + c
         index = jnp.where(first, place, place - 3 - c)
         turn = jnp.where(mine, 2 * n + c, 2 * pair + jnp.where(first, 0, 1))
-        one = jnp.where(index == 0, 7, jnp.where(index == 1, 5, 2))
-        other = jnp.where(index == 0, 1, jnp.where(index == 1, 3, jnp.where(index == 2, 6, 4)))
+        one = jnp.where(index == 0, 2, jnp.where(index == 1, 5, 7))
+        other = jnp.where(index == 0, 6, jnp.where(index == 1, 3, jnp.where(index == 2, 1, 4)))
         k = jnp.where(mine, 0, jnp.where((turn + c) % 2 == 0, one, other))
         slot = jnp.where(turn == 8, 32 + k // 2, 4 * k + turn // 2)
         return k, tile_of(turn), slot

time: 96.2 us -> 96.3 us (level)
  no operation moved by 1% of the time
where the time goes in v5:
time: 96.3 us; the launch traced here: 95.6 us
  Pallas kernels  95 us (99%)
    pallas_call x1, Pallas kernels, body(): pl.pallas_call(kernel, name='merge_and_place', out_shape=(jax.ShapeDtypeS...  93.1 us

profile of v5, /device:TPU:1, one launch (start us, length us, event | category | flops | bytes accessed | tf_op | source)
XLA Modules:
  0.0 95.6 jit_solution(3820540041562579507)
XLA Ops:
  0.6 93.1 %merge_and_place.1 = (bf16[3,48,12288]{2,1,0:T(8,128)(2,1)S(1)}, f32[1,48]{1,0:T(1,128)S(1)}, f32[1,48]{1,0:T(1,128)S(1)}, f32[1,48]{1,0:T(1,128)S(1)}, bf16[96,128]{1,0:T(8,128)(2,1)S(1)}) custom-call(bf16[192,3072]{1,0:T(8,128)(2,1)} %wq.1, bf16[64,192]{1,0:T(8,128)(2,1)} %bitcast.12, bf16[64,3072]{1,0:T(8,128)(2,1)} %hq.1, bf16[192,3072]{1,0:T(8,128)(2,1)} %wk.1, ...), custom_call_target="tpu_custom_call" | custom-call | tf_op jit(solution)/shard_map/merge_and_place/pallas_call | solution.py:403
  93.7 1.9 %settle.1 = (bf16[48,12288]{1,0:T(8,128)(2,1)}, bf16[48,12288]{1,0:T(8,128)(2,1)}, bf16[48,12288]{1,0:T(8,128)(2,1)}, f32[1,48]{1,0:T(1,128)}, f32[1,48]{1,0:T(1...) custom-call(bf16[3,48,12288]{2,1,0:T(8,128)(2,1)S(1)} %get-tuple-element.19.out, f32[1,48]{1,0:T(1,128)S(1)} %get-tuple-element.20.cq, ...), custom_call_target="tpu_custom_call" | custom-call | tf_op jit(solution)/shard_map/settle/pallas_call | solution.py:438
